TPU v7x, 32 devices: a whole 2x2x4 slice. The times are simulated.
32 devices in a mesh: lat: 8 (over z, y), rad: 4 (over x, core).
Axes of the slice: x: 2, y: 2, z: 4, core: 2. Of those that a mesh axis runs over, the one named last changes fastest.
Arguments:
- displacement: float32 [64, 6144], P('rad', 'lat'), may hold values from -6 to 6
- surface_load: float32 [64, 6144], P('rad', 'lat'), may hold values from -6 to 6
- dens_grad: float32 [64, 6144], P('rad', 'lat'), may hold values from 0.5 to 2
- dens_ref: float32 [64], P('rad'), may hold values from 0.5 to 2
- relax_rate: float32 [64, 6144], P('rad', 'lat'), may hold values from 0.02 to 0.2
- basis: bfloat16 [2408, 6144], P(None, 'lat'), may hold values from -0.109375 to 0.109375
- neighbours: int32 [4, 6144], P(None, 'lat'), may hold values from 0 to 767
- green: float32 [49, 64, 64], replicated, may hold values from -2.5 to 2.5
Outputs:
- relaxed: float32 [64, 6144], P('rad', 'lat')
- step_sizes: float32 [3], replicated
Inputs may be any that keep to these rules, and one draw needn't show every extreme that they name: `neighbours`: indices of columns inside the same tile of 768 columns.
All inputs are finite; a program needn't handle non-finite values.
Results may differ from a plain program's by a relative error of at most 0.0045.
Values may be sent and summed in bfloat16 or wider, within the bound.
No kernel may reach another device: no remote copies, remote signals or barrier semaphores. Data moves between devices by JAX's collectives and lax.ppermute only.
A program may use at most 64 MiB of HBM per device.

v0:
```python
import jax
import jax.numpy as jnp
from jax import lax
from jax.sharding import PartitionSpec as P

DEG = 48
L = 64
ITERS = 3
KH = 2401


def extended(shard, sides, width):
    for axis, dim in sides:
        size, length = (lax.axis_size(axis), shard.shape[dim])
        up = [(i, (i + 1) % size) for i in range(size - 1)]
        down = [(j, i) for i, j in up]
        last = lax.slice_in_dim(shard, length - width, length, axis=dim)
        first = lax.slice_in_dim(shard, 0, width, axis=dim)
        before = lax.ppermute(last, axis, up)
        after = lax.ppermute(first, axis, down)
        shard = jnp.concatenate([before, shard, after], axis=dim)
    return shard


def apply_degrees(coefs, green_rows):
    blocks = []
    for degree in range(DEG + 1):
        rows = coefs[degree * degree : (degree + 1) * (degree + 1)]
        blocks.append(
            lax.dot_general(
                rows,
                green_rows[degree],
                (((1,), (1,)), ((), ())),
                precision=lax.Precision.HIGHEST,
                preferred_element_type=jnp.float32,
            )
        )
    blocks.append(jnp.zeros((coefs.shape[0] - KH, green_rows.shape[1]), jnp.float32))
    return jnp.concatenate(blocks, axis=0).astype(jnp.bfloat16)


def local(displacement, surface_load, dens_grad, dens_ref, relax_rate, basis, neighbours, green):
    u = displacement
    layers, columns = u.shape
    lat_count = lax.axis_size("lat")
    green_rows = lax.dynamic_slice_in_dim(green, lax.axis_index("rad") * layers, layers, 1)
    sizes = []
    for it in range(ITERS):
        padded = extended(u, (("rad", 0),), 1)
        rho = (dens_grad * u + dens_ref[:, None] * (padded[2:] - padded[:-2]) * 0.5).astype(
            jnp.bfloat16
        )
        partial_sums = lax.dot_general(
            basis, rho, (((1,), (1,)), ((), ())), preferred_element_type=jnp.float32
        )
        summed = lax.psum(partial_sums, "lat")
        coefs = lax.all_gather(summed, "rad", axis=1, tiled=True)
        phi = apply_degrees(coefs, green_rows)
        potential = lax.dot_general(
            phi, basis, (((0,), (0,)), ((), ())), preferred_element_type=jnp.float32
        )
        outer = extended(potential, (("rad", 0),), 1)
        force = (outer[2:] - outer[:-2]) * 0.5
        lap = jnp.sum(u[:, neighbours], axis=1) - 4.0 * u
        new = u + relax_rate * (surface_load + force + lap - u)
        squared = jnp.sum((new - u) ** 2)
        sizes.append(squared)
        u = new
    totals = jnp.stack(sizes)
    totals = lax.psum(totals, ("lat", "rad"))
    return (u, jnp.sqrt(totals / (L * columns * lat_count)))


def solution(mesh):
    placed = (
        P("rad", "lat"),
        P("rad", "lat"),
        P("rad", "lat"),
        P("rad"),
        P("rad", "lat"),
        P(None, "lat"),
        P(None, "lat"),
        P(),
    )
    return jax.shard_map(
        local, mesh=mesh, in_specs=placed, out_specs=(P("rad", "lat"), P()), check_vma=False
    )
```

profile of v0, /device:TPU:0, one launch (start us, length us, event | category | flops | bytes accessed | tf_op | source)
XLA Modules:
  0.0 424.7 jit_solution(13441633414190941219)
XLA Ops:
  8.1 2.4 collective-permute-start.1
  11.8 3.8 collective-permute-done
  15.6 3.9 convolution_bitcast_fusion.2
  19.7 72.3 %all-reduce.4.cloned.1.call-done = f32[2408,16]{0,1:T(8,128)} async-done(((f32[2408,16]{0,1:T(8,128)}), f32[2408,16]{0,1:T(8,128)}) %all-reduce.4.cloned.1.call-update) | async-done | bytes 154128 | tf_op jit(solution)/shard_map/psum | solution.py:56
  92.0 7.9 %all_gather.9 = f32[2408,64]{0,1:T(8,128)S(1)} all-gather(f32[2408,16]{0,1:T(8,128)} %all-reduce.4.cloned.1.call-done), channel_id=1, replica_groups=mesh['lat'=8,'rad'=4] {'rad'}, dimensions={1}, use_global_device_ids=true | all-gather | bytes 770560 | tf_op jit(solution)/shard_map/all_gather | solution.py:57
  112.0 2.7 fusion.407
  118.4 10.8 %gather_fusion = f32[3072,16]{1,0:T(8,128)} fusion(f32[16,768]{0,1:T(8,128)S(1)} %copy.24, s32[3072]{0:T(1024)S(1)} %broadcast_clamp_fusion), kind=kCustom, calls=%fused_computation | custom fusion | bytes 405504 | tf_op jit(solution)/shard_map/gather | solution.py:64
  131.1 3.0 collective-permute-start.5
  135.5 2.8 collective-permute-done.4
  138.3 3.8 convolution_bitcast_fusion.1
  142.1 70.9 %all-reduce.6.cloned.1.call-done = f32[2408,16]{0,1:T(8,128)} async-done(((f32[2408,16]{0,1:T(8,128)}), f32[2408,16]{0,1:T(8,128)}) %all-reduce.6.cloned.1.call-update) | async-done | bytes 154128 | tf_op jit(solution)/shard_map/psum | solution.py:56
  213.1 7.9 %all_gather.10 = f32[2408,64]{0,1:T(8,128)S(1)} all-gather(f32[2408,16]{0,1:T(8,128)} %all-reduce.6.cloned.1.call-done), channel_id=1, replica_groups=mesh['lat'=8,'rad'=4] {'rad'}, dimensions={1}, use_global_device_ids=true | all-gather | bytes 770560 | tf_op jit(solution)/shard_map/all_gather | solution.py:57
  233.1 2.6 fusion.408
  235.7 2.3 collective-permute-start.7
  239.4 10.8 %gather_fusion.1 = f32[3072,16]{1,0:T(8,128)} fusion(f32[16,768]{0,1:T(8,128)S(1)} %copy.34, s32[3072]{0:T(1024)S(1)} %broadcast_clamp_fusion), kind=kCustom, calls=%fused_computation.1 | custom fusion | bytes 405504 | tf_op jit(solution)/shard_map/gather | solution.py:64
  252.0 3.0 collective-permute-start.9
  256.4 2.8 collective-permute-done.8
  259.2 3.8 convolution_bitcast_fusion
  263.0 71.0 %all-reduce.8.cloned.1.call-done = f32[2408,16]{0,1:T(8,128)} async-done(((f32[2408,16]{0,1:T(8,128)}), f32[2408,16]{0,1:T(8,128)}) %all-reduce.8.cloned.1.call-update) | async-done | bytes 154128 | tf_op jit(solution)/shard_map/psum | solution.py:56
  334.0 8.1 %all_gather.11 = f32[2408,64]{0,1:T(8,128)S(1)} all-gather(f32[2408,16]{0,1:T(8,128)} %all-reduce.8.cloned.1.call-done), channel_id=1, replica_groups=mesh['lat'=8,'rad'=4] {'rad'}, dimensions={1}, use_global_device_ids=true | all-gather | bytes 770560 | tf_op jit(solution)/shard_map/all_gather | solution.py:57
  354.2 2.6 fusion.409
  356.8 2.3 collective-permute-start.11
  360.6 10.8 %gather_fusion.2 = f32[3072,16]{1,0:T(8,128)} fusion(f32[16,768]{0,1:T(8,128)S(1)} %copy.44, s32[3072]{0:T(1024)S(1)} %broadcast_clamp_fusion), kind=kCustom, calls=%fused_computation.2 | custom fusion | bytes 405504 | tf_op jit(solution)/shard_map/gather | solution.py:64
  376.4 41.3 %psum.31 = f32[3]{0:T(128)S(1)} all-reduce(f32[3]{0:T(128)S(1)} %pad_maximum_fusion.12), channel_id=1, replica_groups=mesh['lat'=8,'rad'=4] {'lat','rad'}, use_global_device_ids=true, to_apply=%region_9.0 | all-reduce | flops 3 | bytes 24 | tf_op jit(solution)/shard_map/psum | solution.py:70
  (237 shorter events, 56.8 us)
Async XLA Ops:
  7.2 92.8 %copy-start = (f32[49,64,64]{2,1,0:T(8,128)S(1)}, f32[49,64,64]{2,1,0:T(8,128)}, u32[]{:S(2)}) copy-start(f32[49,64,64]{2,1,0:T(8,128)} %param.15) | copy-start | bytes 2408452
  7.2 84.8 %all-reduce.4.cloned.1.call-start = ((), (), s32[]{:S(2)}) async-start(), calls=%async_computation | async-start | bytes 311296 | tf_op jit(solution)/shard_map/psum | solution.py:56
  8.1 3.7 collective-permute-start.1
  10.5 5.2 %collective-permute-start = (f32[1,768]{1,0:T(1,128)S(1)}, f32[1,768]{1,0:T(1,128)S(1)}, u32[]{:S(2)}, u32[]{:S(2)}) collective-permute-start(f32[1,768]{1,0:T(1,128)S(1)} %get-tuple-element.16), channel_id=1, source_target_pairs={{1,0},{2,1},{3,2},{5,4},{6,5},{7,6},{9,8},{10,9},{11,10},{13,12},{... | collective-permute-start | bytes 9224 | tf_op jit(solution)/shard_map/ppermute | solution.py:20
  11.8 7.8 %copy-start.5 = (s32[4,768]{1,0:T(4,128)S(1)}, s32[4,768]{1,0:T(4,128)}, u32[]{:S(2)}) copy-start(s32[4,768]{1,0:T(4,128)} %param.14) | copy-start | bytes 36868
  19.6 193.5 %all-reduce.6.cloned.1.call-start = ((), (), s32[]{:S(2)}) async-start(), calls=%async_computation.1 | async-start | bytes 311296 | tf_op jit(solution)/shard_map/psum | solution.py:56
  112.0 6.3 %copy-start.1 = (f32[16,768]{1,0:T(8,128)S(1)}, f32[16,768]{1,0:T(8,128)}, u32[]{:S(2)}) copy-start(f32[16,768]{1,0:T(8,128)} %param.8) | copy-start | bytes 147460
  114.7 16.3 %collective-permute-start.3 = (f32[1,768]{1,0:T(1,128)S(1)}, f32[1,768]{1,0:T(1,128)S(1)}, u32[]{:S(2)}, u32[]{:S(2)}) collective-permute-start(f32[1,768]{1,0:T(1,128)S(1)} %get-tuple-element.15), channel_id=1, source_target_pairs={{0,1},{1,2},{2,3},{4,5},{5,6},{6,7},{8,9},{9,10},{10,11},{12,13},{... | collective-permute-start | bytes 9224 | tf_op jit(solution)/shard_map/ppermute | solution.py:19
  116.9 14.1 %collective-permute-start.2 = (f32[1,768]{1,0:T(1,128)S(1)}, f32[1,768]{1,0:T(1,128)S(1)}, u32[]{:S(2)}, u32[]{:S(2)}) collective-permute-start(f32[1,768]{1,0:T(1,128)S(1)} %get-tuple-element.14), channel_id=1, source_target_pairs={{1,0},{2,1},{3,2},{5,4},{6,5},{7,6},{9,8},{10,9},{11,10},{13,12},{... | collective-permute-start | bytes 9224 | tf_op jit(solution)/shard_map/ppermute | solution.py:20
  129.3 1.8 copy-start.3
  129.3 1.8 copy-start.4
  129.3 9.0 %copy-start.2 = (f32[16,768]{1,0:T(8,128)S(1)}, f32[16,768]{1,0:T(8,128)}, u32[]{:S(2)}) copy-start(f32[16,768]{1,0:T(8,128)} %param.10) | copy-start | bytes 147460
  129.3 9.0 %copy-start.6 = (f32[16]{0:T(128)S(1)}, f32[16]{0:T(128)}, u32[]{:S(2)}) copy-start(f32[16]{0:T(128)} %param.11) | copy-start | bytes 196
  131.1 4.3 %collective-permute-start.5 = (f32[1,768]{1,0:T(1,128)S(1)}, f32[1,768]{1,0:T(1,128)S(1)}, u32[]{:S(2)}, u32[]{:S(2)}) collective-permute-start(f32[1,768]{1,0:T(1,128)S(1)} %get-tuple-element.13), channel_id=1, source_target_pairs={{0,1},{1,2},{2,3},{4,5},{5,6},{6,7},{8,9},{9,10},{10,11},{12,13},{... | collective-permute-start | bytes 9224 | tf_op jit(solution)/shard_map/ppermute | solution.py:19
  134.1 4.1 collective-permute-start.4
  142.1 191.9 %all-reduce.8.cloned.1.call-start = ((), (), s32[]{:S(2)}) async-start(), calls=%async_computation.2 | async-start | bytes 311296 | tf_op jit(solution)/shard_map/psum | solution.py:56
  235.7 16.2 %collective-permute-start.7 = (f32[1,768]{1,0:T(1,128)S(1)}, f32[1,768]{1,0:T(1,128)S(1)}, u32[]{:S(2)}, u32[]{:S(2)}) collective-permute-start(f32[1,768]{1,0:T(1,128)S(1)} %get-tuple-element.11), channel_id=1, source_target_pairs={{0,1},{1,2},{2,3},{4,5},{5,6},{6,7},{8,9},{9,10},{10,11},{12,13},{... | collective-permute-start | bytes 9224 | tf_op jit(solution)/shard_map/ppermute | solution.py:19
  238.0 14.0 %collective-permute-start.6 = (f32[1,768]{1,0:T(1,128)S(1)}, f32[1,768]{1,0:T(1,128)S(1)}, u32[]{:S(2)}, u32[]{:S(2)}) collective-permute-start(f32[1,768]{1,0:T(1,128)S(1)} %get-tuple-element.10), channel_id=1, source_target_pairs={{1,0},{2,1},{3,2},{5,4},{6,5},{7,6},{9,8},{10,9},{11,10},{13,12},{... | collective-permute-start | bytes 9224 | tf_op jit(solution)/shard_map/ppermute | solution.py:20
  252.0 4.3 %collective-permute-start.9 = (f32[1,768]{1,0:T(1,128)S(1)}, f32[1,768]{1,0:T(1,128)S(1)}, u32[]{:S(2)}, u32[]{:S(2)}) collective-permute-start(f32[1,768]{1,0:T(1,128)S(1)} %get-tuple-element.9), channel_id=1, source_target_pairs={{0,1},{1,2},{2,3},{4,5},{5,6},{6,7},{8,9},{9,10},{10,11},{12,13},{... | collective-permute-start | bytes 9224 | tf_op jit(solution)/shard_map/ppermute | solution.py:19
  255.1 4.1 collective-permute-start.8
  356.8 16.2 %collective-permute-start.11 = (f32[1,768]{1,0:T(1,128)S(1)}, f32[1,768]{1,0:T(1,128)S(1)}, u32[]{:S(2)}, u32[]{:S(2)}) collective-permute-start(f32[1,768]{1,0:T(1,128)S(1)} %get-tuple-element.7), channel_id=1, source_target_pairs={{0,1},{1,2},{2,3},{4,5},{5,6},{6,7},{8,9},{9,10},{10,11},{12,13},{... | collective-permute-start | bytes 9224 | tf_op jit(solution)/shard_map/ppermute | solution.py:19
  359.1 14.0 %collective-permute-start.10 = (f32[1,768]{1,0:T(1,128)S(1)}, f32[1,768]{1,0:T(1,128)S(1)}, u32[]{:S(2)}, u32[]{:S(2)}) collective-permute-start(f32[1,768]{1,0:T(1,128)S(1)} %get-tuple-element.6), channel_id=1, source_target_pairs={{1,0},{2,1},{3,2},{5,4},{6,5},{7,6},{9,8},{10,9},{11,10},{13,12},{... | collective-permute-start | bytes 9224 | tf_op jit(solution)/shard_map/ppermute | solution.py:20
Sparse Core Ops, SparseCore 0:
  19.7 72.2 all-reduce.3
  142.2 70.8 all-reduce.5
  263.1 70.8 all-reduce.7
where the time goes:
time: 426 us; the launch traced here: 425 us
  waiting for transfers between devices  224 us (53%)
  blocking collectives  65.1 us (15%)
  matrix products  52.3 us (12%)
  local copies, waits for them, and re-layouts  37.5 us (9%)
  starting transfers between devices  23.1 us (5%)
  between operations  14.2 us (3%)
  other arithmetic  8.64 us (2%)
    psum x3, waiting for transfers between devices, local(): summed = lax.psum(partial_sums, 'lat')  214 us
    psum x1, blocking collectives, local(): totals = lax.psum(totals, ('lat', 'rad'))  41.3 us
    dot_general x147, matrix products, apply_degrees(): lax.dot_general(rows, green_rows[degree], (((1,), (1,)), ((), ())), preci...  32.9 us
    gather x3, local copies, waits for them, and re-layouts, local(): lap = jnp.sum(u[:, neighbours], axis=1) - 4.0 * u  32.5 us
    all_gather x3, blocking collectives, local(): coefs = lax.all_gather(summed, 'rad', axis=1, tiled=True)  23.9 us
    ppermute x6, starting transfers between devices, extended(): before = lax.ppermute(last, axis, up)  15.2 us
    dot_general x3, matrix products, local(): lax.dot_general(basis, rho, (((1,), (1,)), ((), ())), preferred_element_t...  11.5 us
    ppermute x6, waiting for transfers between devices, extended(): after = lax.ppermute(first, axis, down)  9.47 us
  transfers between devices with their start and end apart: 15, of which 6 were waited for; matrix products, arithmetic and copies ran while one was open for 9% of the time, Pallas kernels for 0%

commit v1 on v0

--- a/solution.py
+++ b/solution.py
@@ -53,7 +53,7 @@
         partial_sums = lax.dot_general(
             basis, rho, (((1,), (1,)), ((), ())), preferred_element_type=jnp.float32
         )
-        summed = lax.psum(partial_sums, "lat")
+        summed = jnp.sum(jax.lax.all_gather(partial_sums, "lat"), 0)
         coefs = lax.all_gather(summed, "rad", axis=1, tiled=True)
         phi = apply_degrees(coefs, green_rows)
         potential = lax.dot_general(

time: 426 us -> 340 us (0.80)
  waiting for transfers between devices: 224 us -> 137 us
    psum x3 -> x0, waiting for transfers between devices: 214 us -> none  [local(): summed = lax.psum(partial_sums, 'lat')]
    all_gather x0 -> x3, waiting for transfers between devices: none -> 127 us  [local(): summed = jnp.sum(jax.lax.all_gather(partial_sums, 'lat'), 0)]
  transfers between devices with their start and end apart: 15 -> 15, of which waited for: 6 -> 6; matrix products, arithmetic and copies ran while one was open for 9% -> 11% of each run, Pallas kernels for 0% -> 0%
where the time goes in v1:
time: 340 us; the launch traced here: 339 us
  waiting for transfers between devices  137 us (40%)
  blocking collectives  62.9 us (18%)
  matrix products  52.4 us (15%)
  local copies, waits for them, and re-layouts  37.5 us (11%)
  starting transfers between devices  23.1 us (7%)
  between operations  14.2 us (4%)
  other arithmetic  12.8 us (4%)
    all_gather x3, waiting for transfers between devices, local(): summed = jnp.sum(jax.lax.all_gather(partial_sums, 'lat'), 0)  127 us
    psum x1, blocking collectives, local(): totals = lax.psum(totals, ('lat', 'rad'))  39.7 us
    dot_general x147, matrix products, apply_degrees(): lax.dot_general(rows, green_rows[degree], (((1,), (1,)), ((), ())), preci...  32.9 us
    gather x3, local copies, waits for them, and re-layouts, local(): lap = jnp.sum(u[:, neighbours], axis=1) - 4.0 * u  32.5 us
    all_gather x3, blocking collectives, local(): coefs = lax.all_gather(summed, 'rad', axis=1, tiled=True)  23.2 us
    ppermute x6, starting transfers between devices, extended(): before = lax.ppermute(last, axis, up)  15.2 us
    dot_general x3, matrix products, local(): lax.dot_general(basis, rho, (((1,), (1,)), ((), ())), preferred_element_t...  11.5 us
    ppermute x6, waiting for transfers between devices, extended(): after = lax.ppermute(first, axis, down)  9.49 us
  transfers between devices with their start and end apart: 15, of which 6 were waited for; matrix products, arithmetic and copies ran while one was open for 11% of the time, Pallas kernels for 0%

profile of v1, /device:TPU:0, one launch (start us, length us, event | category | flops | bytes accessed | tf_op | source)
XLA Modules:
  0.0 339.3 jit_solution(2313997748299436491)
XLA Ops:
  8.1 2.4 collective-permute-start.1
  11.8 3.8 %collective-permute-done = f32[1,768]{1,0:T(1,128)S(1)} collective-permute-done((f32[1,768]{1,0:T(1,128)S(1)}, f32[1,768]{1,0:T(1,128)S(1)}, u32[]{:S(2)}, u32[]{:S(2)}) %collective-permute-start) | collective-permute-done | bytes 3104 | tf_op jit(solution)/shard_map/ppermute | solution.py:20
  15.7 3.9 %convolution_bitcast_fusion.2 = f32[1,2408,16]{1,2,0:T(8,128)} fusion(bf16[2408,768]{1,0:T(8,128)(2,1)} %param.13, f32[16,768]{1,0:T(8,128)} %param.8, f32[1,768]{1,0:T(1,128)S(1)} %collective-permute-done.1, f32[1,768]{1,0:T(1,128)S(1)} %collective-permute-done, f32[16,768]{1,0:T(8,128)} %param.10, f32[16]{0:T(128)} %param.11), kind=kOutput, calls=%fused_computation.5 | convolution fusion | flops 59277312 | bytes 3957312 | tf_op jit(solution)/shard_map/dot_general | solution.py:53
  19.7 43.9 %all-gather.10.cloned.1.call-done = f32[8,2408,16]{1,2,0:T(8,128)} async-done(((f32[1,2408,16]{1,2,0:T(8,128)}), f32[8,2408,16]{1,2,0:T(8,128)}) %all-gather.10.cloned.1.call-update) | async-done | bytes 1232912 | tf_op jit(solution)/shard_map/all_gather | solution.py:56
  65.0 7.7 %all_gather.29 = f32[2408,64]{0,1:T(8,128)S(1)} all-gather(f32[2408,16]{0,1:T(8,128)S(1)} %reduce_sum.81), channel_id=1, replica_groups=mesh['lat'=8,'rad'=4] {'rad'}, dimensions={1}, use_global_device_ids=true | all-gather | bytes 770560 | tf_op jit(solution)/shard_map/all_gather | solution.py:57
  84.8 2.7 fusion.407
  87.5 2.3 collective-permute-start.3
  91.2 10.8 %gather_fusion = f32[3072,16]{1,0:T(8,128)} fusion(f32[16,768]{0,1:T(8,128)S(1)} %copy.30, s32[3072]{0:T(1024)S(1)} %broadcast_clamp_fusion), kind=kCustom, calls=%fused_computation | custom fusion | bytes 405504 | tf_op jit(solution)/shard_map/gather | solution.py:64
  103.9 3.0 collective-permute-start.5
  108.3 2.8 collective-permute-done.4
  111.1 3.8 %convolution_bitcast_fusion.1 = f32[1,2408,16]{1,2,0:T(8,128)} fusion(bf16[2408,768]{1,0:T(8,128)(2,1)} %param.13, f32[16,768]{1,0:T(8,128)S(1)} %fusion.36, f32[1,768]{1,0:T(1,128)S(1)} %collective-permute-done.5, f32[1,768]{1,0:T(1,128)S(1)} %collective-permute-done.4, f32[16,768]{1,0:T(8,128)S(1)} %copy-done.2, f32[16]{0:T(128)S(1)} %copy-done.6), kind=kOutput, calls=%fused_computation.4 | convolution fusion | flops 59277312 | bytes 3957312 | tf_op jit(solution)/shard_map/dot_general | solution.py:53
  114.9 41.5 %all-gather.12.cloned.1.call-done = f32[8,2408,16]{1,2,0:T(8,128)} async-done(((f32[1,2408,16]{1,2,0:T(8,128)}), f32[8,2408,16]{1,2,0:T(8,128)}) %all-gather.12.cloned.1.call-update) | async-done | bytes 1232912 | tf_op jit(solution)/shard_map/all_gather | solution.py:56
  157.8 7.7 %all_gather.32 = f32[2408,64]{0,1:T(8,128)S(1)} all-gather(f32[2408,16]{0,1:T(8,128)S(1)} %reduce_sum.83), channel_id=1, replica_groups=mesh['lat'=8,'rad'=4] {'rad'}, dimensions={1}, use_global_device_ids=true | all-gather | bytes 770560 | tf_op jit(solution)/shard_map/all_gather | solution.py:57
  177.6 2.6 fusion.408
  184.0 10.8 %gather_fusion.1 = f32[3072,16]{1,0:T(8,128)} fusion(f32[16,768]{0,1:T(8,128)S(1)} %copy.40, s32[3072]{0:T(1024)S(1)} %broadcast_clamp_fusion), kind=kCustom, calls=%fused_computation.1 | custom fusion | bytes 405504 | tf_op jit(solution)/shard_map/gather | solution.py:64
  196.6 3.0 collective-permute-start.9
  200.9 2.8 collective-permute-done.8
  203.7 3.8 %convolution_bitcast_fusion = f32[1,2408,16]{1,2,0:T(8,128)} fusion(bf16[2408,768]{1,0:T(8,128)(2,1)} %param.13, f32[16,768]{1,0:T(8,128)S(1)} %fusion.24, f32[1,768]{1,0:T(1,128)S(1)} %collective-permute-done.9, f32[1,768]{1,0:T(1,128)S(1)} %collective-permute-done.8, f32[16,768]{1,0:T(8,128)S(1)} %copy-done.2, f32[16]{0:T(128)S(1)} %copy-done.6), kind=kOutput, calls=%fused_computation.3 | convolution fusion | flops 59277312 | bytes 3957312 | tf_op jit(solution)/shard_map/dot_general | solution.py:53
  207.5 41.5 %all-gather.14.cloned.1.call-done = f32[8,2408,16]{1,2,0:T(8,128)} async-done(((f32[1,2408,16]{1,2,0:T(8,128)}), f32[8,2408,16]{1,2,0:T(8,128)}) %all-gather.14.cloned.1.call-update) | async-done | bytes 1232912 | tf_op jit(solution)/shard_map/all_gather | solution.py:56
  250.4 7.9 %all_gather.35 = f32[2408,64]{0,1:T(8,128)S(1)} all-gather(f32[2408,16]{0,1:T(8,128)S(1)} %reduce_sum.85), channel_id=1, replica_groups=mesh['lat'=8,'rad'=4] {'rad'}, dimensions={1}, use_global_device_ids=true | all-gather | bytes 770560 | tf_op jit(solution)/shard_map/all_gather | solution.py:57
  270.4 2.6 fusion.409
  273.1 2.3 collective-permute-start.11
  276.8 10.8 %gather_fusion.2 = f32[3072,16]{1,0:T(8,128)} fusion(f32[16,768]{0,1:T(8,128)S(1)} %copy.50, s32[3072]{0:T(1024)S(1)} %broadcast_clamp_fusion), kind=kCustom, calls=%fused_computation.2 | custom fusion | bytes 405504 | tf_op jit(solution)/shard_map/gather | solution.py:64
  292.6 39.7 %psum.7 = f32[3]{0:T(128)S(1)} all-reduce(f32[3]{0:T(128)S(1)} %pad_maximum_fusion.12), channel_id=1, replica_groups=mesh['lat'=8,'rad'=4] {'lat','rad'}, use_global_device_ids=true, to_apply=%region_9.0 | all-reduce | flops 3 | bytes 24 | tf_op jit(solution)/shard_map/psum | solution.py:70
  (240 shorter events, 60.9 us)
Async XLA Ops:
  7.2 65.6 %copy-start = (f32[49,64,64]{2,1,0:T(8,128)S(1)}, f32[49,64,64]{2,1,0:T(8,128)}, u32[]{:S(2)}) copy-start(f32[49,64,64]{2,1,0:T(8,128)} %param.15) | copy-start | bytes 2408452
  7.2 56.5 %all-gather.10.cloned.1.call-start = ((), (), s32[]{:S(2)}) async-start(), calls=%async_computation | async-start | bytes 1400832 | tf_op jit(solution)/shard_map/all_gather | solution.py:56
  8.1 3.7 %collective-permute-start.1 = (f32[1,768]{1,0:T(1,128)S(1)}, f32[1,768]{1,0:T(1,128)S(1)}, u32[]{:S(2)}, u32[]{:S(2)}) collective-permute-start(f32[1,768]{1,0:T(1,128)S(1)} %get-tuple-element.17), channel_id=1, source_target_pairs={{0,1},{1,2},{2,3},{4,5},{5,6},{6,7},{8,9},{9,10},{10,11},{12,13},{... | collective-permute-start | bytes 9224 | tf_op jit(solution)/shard_map/ppermute | solution.py:19
  10.5 9.2 %copy-start.5 = (s32[4,768]{1,0:T(4,128)S(1)}, s32[4,768]{1,0:T(4,128)}, u32[]{:S(2)}) copy-start(s32[4,768]{1,0:T(4,128)} %param.14) | copy-start | bytes 36868
  10.5 5.2 %collective-permute-start = (f32[1,768]{1,0:T(1,128)S(1)}, f32[1,768]{1,0:T(1,128)S(1)}, u32[]{:S(2)}, u32[]{:S(2)}) collective-permute-start(f32[1,768]{1,0:T(1,128)S(1)} %get-tuple-element.16), channel_id=1, source_target_pairs={{1,0},{2,1},{3,2},{5,4},{6,5},{7,6},{9,8},{10,9},{11,10},{13,12},{... | collective-permute-start | bytes 9224 | tf_op jit(solution)/shard_map/ppermute | solution.py:20
  19.6 136.8 %all-gather.12.cloned.1.call-start = ((), (), s32[]{:S(2)}) async-start(), calls=%async_computation.1 | async-start | bytes 1400832 | tf_op jit(solution)/shard_map/all_gather | solution.py:56
  84.8 6.3 %copy-start.1 = (f32[16,768]{1,0:T(8,128)S(1)}, f32[16,768]{1,0:T(8,128)}, u32[]{:S(2)}) copy-start(f32[16,768]{1,0:T(8,128)} %param.8) | copy-start | bytes 147460
  87.5 16.3 %collective-permute-start.3 = (f32[1,768]{1,0:T(1,128)S(1)}, f32[1,768]{1,0:T(1,128)S(1)}, u32[]{:S(2)}, u32[]{:S(2)}) collective-permute-start(f32[1,768]{1,0:T(1,128)S(1)} %get-tuple-element.15), channel_id=1, source_target_pairs={{0,1},{1,2},{2,3},{4,5},{5,6},{6,7},{8,9},{9,10},{10,11},{12,13},{... | collective-permute-start | bytes 9224 | tf_op jit(solution)/shard_map/ppermute | solution.py:19
  89.8 14.1 %collective-permute-start.2 = (f32[1,768]{1,0:T(1,128)S(1)}, f32[1,768]{1,0:T(1,128)S(1)}, u32[]{:S(2)}, u32[]{:S(2)}) collective-permute-start(f32[1,768]{1,0:T(1,128)S(1)} %get-tuple-element.14), channel_id=1, source_target_pairs={{1,0},{2,1},{3,2},{5,4},{6,5},{7,6},{9,8},{10,9},{11,10},{13,12},{... | collective-permute-start | bytes 9224 | tf_op jit(solution)/shard_map/ppermute | solution.py:20
  102.1 1.8 copy-start.3
  102.1 1.8 copy-start.4
  102.1 9.0 %copy-start.2 = (f32[16,768]{1,0:T(8,128)S(1)}, f32[16,768]{1,0:T(8,128)}, u32[]{:S(2)}) copy-start(f32[16,768]{1,0:T(8,128)} %param.10) | copy-start | bytes 147460
  102.1 9.0 %copy-start.6 = (f32[16]{0:T(128)S(1)}, f32[16]{0:T(128)}, u32[]{:S(2)}) copy-start(f32[16]{0:T(128)} %param.11) | copy-start | bytes 196
  103.9 4.3 %collective-permute-start.5 = (f32[1,768]{1,0:T(1,128)S(1)}, f32[1,768]{1,0:T(1,128)S(1)}, u32[]{:S(2)}, u32[]{:S(2)}) collective-permute-start(f32[1,768]{1,0:T(1,128)S(1)} %get-tuple-element.13), channel_id=1, source_target_pairs={{0,1},{1,2},{2,3},{4,5},{5,6},{6,7},{8,9},{9,10},{10,11},{12,13},{... | collective-permute-start | bytes 9224 | tf_op jit(solution)/shard_map/ppermute | solution.py:19
  107.0 4.1 %collective-permute-start.4 = (f32[1,768]{1,0:T(1,128)S(1)}, f32[1,768]{1,0:T(1,128)S(1)}, u32[]{:S(2)}, u32[]{:S(2)}) collective-permute-start(f32[1,768]{1,0:T(1,128)S(1)} %get-tuple-element.12), channel_id=1, source_target_pairs={{1,0},{2,1},{3,2},{5,4},{6,5},{7,6},{9,8},{10,9},{11,10},{13,12},{... | collective-permute-start | bytes 9224 | tf_op jit(solution)/shard_map/ppermute | solution.py:20
  114.9 134.2 %all-gather.14.cloned.1.call-start = ((), (), s32[]{:S(2)}) async-start(), calls=%async_computation.2 | async-start | bytes 1400832 | tf_op jit(solution)/shard_map/all_gather | solution.py:56
  180.2 16.2 %collective-permute-start.7 = (f32[1,768]{1,0:T(1,128)S(1)}, f32[1,768]{1,0:T(1,128)S(1)}, u32[]{:S(2)}, u32[]{:S(2)}) collective-permute-start(f32[1,768]{1,0:T(1,128)S(1)} %get-tuple-element.11), channel_id=1, source_target_pairs={{0,1},{1,2},{2,3},{4,5},{5,6},{6,7},{8,9},{9,10},{10,11},{12,13},{... | collective-permute-start | bytes 9224 | tf_op jit(solution)/shard_map/ppermute | solution.py:19
  182.5 14.0 %collective-permute-start.6 = (f32[1,768]{1,0:T(1,128)S(1)}, f32[1,768]{1,0:T(1,128)S(1)}, u32[]{:S(2)}, u32[]{:S(2)}) collective-permute-start(f32[1,768]{1,0:T(1,128)S(1)} %get-tuple-element.10), channel_id=1, source_target_pairs={{1,0},{2,1},{3,2},{5,4},{6,5},{7,6},{9,8},{10,9},{11,10},{13,12},{... | collective-permute-start | bytes 9224 | tf_op jit(solution)/shard_map/ppermute | solution.py:20
  196.6 4.3 %collective-permute-start.9 = (f32[1,768]{1,0:T(1,128)S(1)}, f32[1,768]{1,0:T(1,128)S(1)}, u32[]{:S(2)}, u32[]{:S(2)}) collective-permute-start(f32[1,768]{1,0:T(1,128)S(1)} %get-tuple-element.9), channel_id=1, source_target_pairs={{0,1},{1,2},{2,3},{4,5},{5,6},{6,7},{8,9},{9,10},{10,11},{12,13},{... | collective-permute-start | bytes 9224 | tf_op jit(solution)/shard_map/ppermute | solution.py:19
  199.6 4.1 %collective-permute-start.8 = (f32[1,768]{1,0:T(1,128)S(1)}, f32[1,768]{1,0:T(1,128)S(1)}, u32[]{:S(2)}, u32[]{:S(2)}) collective-permute-start(f32[1,768]{1,0:T(1,128)S(1)} %get-tuple-element.8), channel_id=1, source_target_pairs={{1,0},{2,1},{3,2},{5,4},{6,5},{7,6},{9,8},{10,9},{11,10},{13,12},{... | collective-permute-start | bytes 9224 | tf_op jit(solution)/shard_map/ppermute | solution.py:20
  273.1 16.2 %collective-permute-start.11 = (f32[1,768]{1,0:T(1,128)S(1)}, f32[1,768]{1,0:T(1,128)S(1)}, u32[]{:S(2)}, u32[]{:S(2)}) collective-permute-start(f32[1,768]{1,0:T(1,128)S(1)} %get-tuple-element.7), channel_id=1, source_target_pairs={{0,1},{1,2},{2,3},{4,5},{5,6},{6,7},{8,9},{9,10},{10,11},{12,13},{... | collective-permute-start | bytes 9224 | tf_op jit(solution)/shard_map/ppermute | solution.py:19
  275.3 14.0 %collective-permute-start.10 = (f32[1,768]{1,0:T(1,128)S(1)}, f32[1,768]{1,0:T(1,128)S(1)}, u32[]{:S(2)}, u32[]{:S(2)}) collective-permute-start(f32[1,768]{1,0:T(1,128)S(1)} %get-tuple-element.6), channel_id=1, source_target_pairs={{1,0},{2,1},{3,2},{5,4},{6,5},{7,6},{9,8},{10,9},{11,10},{13,12},{... | collective-permute-start | bytes 9224 | tf_op jit(solution)/shard_map/ppermute | solution.py:20
Sparse Core Ops, SparseCore 0:
  19.7 43.8 all-gather.9
  115.0 41.3 all-gather.11
  207.7 41.3 all-gather.13
